TPU v7x, 32 devices: a whole 2x2x4 slice. The times are simulated.
32 devices in a mesh: band: 16 (over z, y, core), ga: 2 (over x).
Axes of the slice: x: 2, y: 2, z: 4, core: 2. Of those that a mesh axis runs over, the one named last changes fastest.
Arguments:
- orbitals: bfloat16 [2, 16, 160, 128], P(None, 'band', 'ga'), may hold values from -8 to 8, as said below
- potential: float32 [480, 480], P('ga'), may hold values from -2 to 2
- slot_sticks: int32 [160], replicated, may hold values from -1 to 126, as said below
- stick_entries: int32 [160, 128], replicated, may hold values from -1 to 126, as said below
Outputs:
- applied_orbitals: bfloat16 [2, 16, 160, 128], P(None, 'band', 'ga')
- correlation: float32 [2, 16, 16], replicated
- reduced_hamiltonian: float32 [2, 16, 16], replicated
Inputs may be any that keep to these rules, and one draw needn't show every extreme that they name: `slot_sticks`: every gx with |gx| < 64 is held by exactly one slot; the other slots hold -1. Slots t with t // 80 = d are those of index d of ga; on some index of ga all 80 slots hold sticks. `stick_entries`: row t lists, in some order, gz + 63 for every gz with gx^2 + gz^2 < 64^2, gx being the stick of slot t, then -1 to the end of the row; rows of empty slots are all -1. `orbitals`: entries where stick_entries is -1 carry values that are not used.
All inputs are finite; a program needn't handle non-finite values.
Results may differ from a plain program's by a relative error of at most 0.001.
Values may be sent and summed in bfloat16 or wider, within the bound.
A program may use at most 64 MiB of HBM per device.

v0:
```python
import jax
import jax.numpy as jnp
from jax import lax
from jax.sharding import PartitionSpec as P

TWO_PI = 6.283185307179586
HIGHEST_PRECISION = lax.Precision.HIGHEST


def phases(frequency, position, points):
    winding = frequency[:, None] * position[None, :] % points
    angles = winding.astype(jnp.float32) * (TWO_PI / points)
    return (jnp.cos(angles), jnp.sin(angles))


def stick_phases(slot_sticks, radius, points):
    frequency = slot_sticks - radius + 1
    x_cos, x_sin = phases(frequency, jnp.arange(points, dtype=jnp.int32), points)
    filled = (slot_sticks >= 0).astype(jnp.float32)[:, None]
    return (x_cos * filled, x_sin * filled)


def selector_table(entry_lists):
    width = entry_lists.shape[1]
    return (entry_lists[:, :, None] == jnp.arange(width, dtype=jnp.int32)[None, None, :]).astype(
        jnp.bfloat16
    )


def spread_entries(coeffs, selector):
    return jnp.einsum("cbsk,skp->cbsp", coeffs, selector, preferred_element_type=jnp.float32)


def pick_entries(spectra, selector):
    return jnp.einsum(
        "cbsp,skp->cbsk", spectra, selector.astype(jnp.float32), precision=HIGHEST_PRECISION
    )


def z_forward(spread, z_cos, z_sin):
    real_part = jnp.einsum(
        "bsp,pz->bsz", spread[0], z_cos, precision=HIGHEST_PRECISION
    ) - jnp.einsum("bsp,pz->bsz", spread[1], z_sin, precision=HIGHEST_PRECISION)
    imag_part = jnp.einsum(
        "bsp,pz->bsz", spread[0], z_sin, precision=HIGHEST_PRECISION
    ) + jnp.einsum("bsp,pz->bsz", spread[1], z_cos, precision=HIGHEST_PRECISION)
    return jnp.stack([real_part, imag_part])


def plane_work(columns, x_cos, x_sin, potential):
    field_real = jnp.einsum(
        "bsz,sx->bzx", columns[0], x_cos, precision=HIGHEST_PRECISION
    ) - jnp.einsum("bsz,sx->bzx", columns[1], x_sin, precision=HIGHEST_PRECISION)
    field_imag = jnp.einsum(
        "bsz,sx->bzx", columns[0], x_sin, precision=HIGHEST_PRECISION
    ) + jnp.einsum("bsz,sx->bzx", columns[1], x_cos, precision=HIGHEST_PRECISION)
    prod_real = potential[None] * field_real
    prod_imag = potential[None] * field_imag
    back_real = jnp.einsum(
        "bzx,sx->bsz", prod_real, x_cos, precision=HIGHEST_PRECISION
    ) + jnp.einsum("bzx,sx->bsz", prod_imag, x_sin, precision=HIGHEST_PRECISION)
    back_imag = jnp.einsum(
        "bzx,sx->bsz", prod_imag, x_cos, precision=HIGHEST_PRECISION
    ) - jnp.einsum("bzx,sx->bsz", prod_real, x_sin, precision=HIGHEST_PRECISION)
    return jnp.stack([back_real, back_imag])


def z_backward(gathered, z_cos, z_sin, points):
    real_part = jnp.einsum(
        "bsz,pz->bsp", gathered[0], z_cos, precision=HIGHEST_PRECISION
    ) + jnp.einsum("bsz,pz->bsp", gathered[1], z_sin, precision=HIGHEST_PRECISION)
    imag_part = jnp.einsum(
        "bsz,pz->bsp", gathered[1], z_cos, precision=HIGHEST_PRECISION
    ) - jnp.einsum("bsz,pz->bsp", gathered[0], z_sin, precision=HIGHEST_PRECISION)
    return jnp.stack([real_part, imag_part]) / float(points * points)


def kinetic_factor(sticks, entry_lists, radius):
    gx_value = sticks - radius + 1
    gz_value = entry_lists - radius + 1
    return ((gx_value * gx_value)[:, None] + gz_value * gz_value).astype(jnp.float32) / float(
        radius * radius
    )


def cross_products(left, right, scale):
    dims = (((1,), (1,)), ((), ()))
    real_part = lax.dot_general(
        left[0], right[0], dims, preferred_element_type=jnp.float32
    ) + lax.dot_general(left[1], right[1], dims, preferred_element_type=jnp.float32)
    imag_part = lax.dot_general(
        left[0], right[1], dims, preferred_element_type=jnp.float32
    ) - lax.dot_general(left[1], right[0], dims, preferred_element_type=jnp.float32)
    return jnp.stack([real_part, imag_part]) * scale


def body(orbitals, potential, slot_sticks, stick_entries):
    points = potential.shape[1]
    width = stick_entries.shape[1]
    radius = width // 2
    band_count = orbitals.shape[1]
    slot_count = orbitals.shape[2]
    ga_index = lax.axis_index("ga")
    own_first = ga_index * slot_count
    own_lists = lax.dynamic_slice_in_dim(stick_entries, own_first, slot_count, 0)
    own_sticks = lax.dynamic_slice_in_dim(slot_sticks, own_first, slot_count, 0)
    present = own_lists >= 0
    own_selector = selector_table(own_lists)
    masked = jnp.where(present[None, None], orbitals, jnp.zeros_like(orbitals))
    frequency = jnp.arange(width, dtype=jnp.int32) - radius + 1
    whole_cos, whole_sin = phases(frequency, jnp.arange(points, dtype=jnp.int32), points)
    x_cos, x_sin = stick_phases(slot_sticks, radius, points)
    columns = z_forward(spread_entries(orbitals, own_selector), whole_cos, whole_sin)
    planes_columns = lax.all_to_all(columns, "ga", split_axis=3, concat_axis=2, tiled=True)
    gathered = plane_work(planes_columns, x_cos, x_sin, potential)
    returned = lax.all_to_all(gathered, "ga", split_axis=2, concat_axis=3, tiled=True)
    spectra = z_backward(returned, whole_cos, whole_sin, points)
    applied = pick_entries(spectra, own_selector)
    kinetic = kinetic_factor(own_sticks, own_lists, radius)
    applied_orbitals = jnp.where(
        present[None, None],
        kinetic[None, None] * orbitals.astype(jnp.float32) + applied,
        jnp.float32(0.0),
    ).astype(jnp.bfloat16)
    scale = 1.0 / (4.0 * radius * radius)
    flat_psi = masked.reshape(2, band_count, -1)
    flat_h = applied_orbitals.reshape(2, band_count, -1)
    portion = lax.all_gather(masked, "band", axis=1, tiled=True)
    remote_psi = portion.reshape(2, portion.shape[1], -1)
    block = jnp.stack(
        [cross_products(remote_psi, flat_psi, scale), cross_products(remote_psi, flat_h, scale)]
    )
    summed = lax.psum(block, "ga")
    matrices = lax.all_gather(summed, "band", axis=3, tiled=True)
    return (applied_orbitals, matrices[0], matrices[1])


def solution(mesh):
    return jax.shard_map(
        body,
        mesh=mesh,
        in_specs=(P(None, "band", "ga", None), P("ga", None), P(), P()),
        out_specs=(P(None, "band", "ga", None), P(), P()),
        check_vma=False,
    )
```

profile of v0, /device:TPU:0, one launch (start us, length us, event | category | flops | bytes accessed | tf_op | source)
XLA Modules:
  0.0 106.6 jit_solution(10663238395581667539)
XLA Ops:
  0.6 0.8 add_multiply_fusion
  1.4 0.9 convert_multiply_fusion
  2.3 3.0 %fusion.10 = f32[2,1,80,128]{3,0,2,1:T(2,128)S(1)} fusion(s32[80,128]{1,0:T(8,128)S(1)} %get-tuple-element.16, bf16[2,80,128]{2,1,0:T(8,128)(2,1)} %bitcast.158), kind=kOutput, calls=%fused_computation.17 | convolution fusion | flops 6553600 | bytes 163840 | tf_op jit(solution)/shard_map/cbsk,skp->cbsp/dot_general | solution.py:31
  5.3 0.1 fusion.194
  5.3 1.3 %fusion.53 = f32[80,480]{1,0:T(8,128)S(1)} fusion(f32[80,128]{1,0:T(8,128)S(1)} %bitcast.156, s32[128]{0:T(128)S(1)} %iota_add_fusion), kind=kOutput, calls=%fused_computation.76 | convolution fusion | flops 59535360 | bytes 195072 | tf_op jit(solution)/shard_map/bsp,pz->bsz/dot_general | solution.py:41
  6.7 1.4 %fusion.57 = f32[80,480]{1,0:T(8,128)S(1)} fusion(f32[80,128]{1,0:T(8,128)S(1)} %bitcast.157, s32[128]{0:T(128)S(1)} %iota_add_fusion), kind=kOutput, calls=%fused_computation.77 | convolution fusion | flops 59535360 | bytes 195072 | tf_op jit(solution)/shard_map/bsp,pz->bsz/dot_general | solution.py:44
  8.1 1.4 %fusion.9 = f32[1,1,80,480]{3,2,1,0:T(8,128)S(1)} fusion(f32[80,480]{1,0:T(8,128)S(1)} %fusion.53, f32[80,128]{1,0:T(8,128)S(1)} %bitcast.154, s32[128]{0:T(128)S(1)} %iota_add_fusion), kind=kOutput, calls=%fused_computation.16 | convolution fusion | flops 59573760 | bytes 348672 | tf_op jit(solution)/shard_map/bsp,pz->bsz/dot_general | solution.py:43
  9.5 1.4 %fusion.8 = f32[1,1,80,480]{3,2,1,0:T(8,128)S(1)} fusion(f32[80,480]{1,0:T(8,128)S(1)} %fusion.57, f32[80,128]{1,0:T(8,128)S(1)} %bitcast.155, s32[128]{0:T(128)S(1)} %iota_add_fusion), kind=kOutput, calls=%fused_computation.14 | convolution fusion | flops 59573760 | bytes 348672 | tf_op jit(solution)/shard_map/bsp,pz->bsz/dot_general | solution.py:46
  10.8 1.0 copy.37
  11.9 0.0 copy-start.2
  11.9 0.0 copy-start.1
  11.9 4.4 %all-to-all-start = ((f32[2,1,80,480]{2,1,0,3:T(1,128)}), f32[2,1,80,480]{2,1,0,3:T(1,128)S(1)}, u32[]{:S(2)}, u32[]{:S(2)}) async-start(f32[2,1,80,480]{2,1,0,3:T(1,128)} %copy.37), calls=%async_computation | async-start | bytes 983040 | tf_op jit(solution)/shard_map/all_to_all | solution.py:114
  16.3 0.0 copy-done.2
  16.3 0.0 copy-done.1
  16.3 0.1 broadcast_select_fusion
  16.4 24.4 %all_gather.6 = bf16[2,16,80,128]{3,2,0,1:T(8,128)(2,1)S(1)} all-gather(bf16[2,1,80,128]{3,2,0,1:T(8,128)(2,1)S(1)} %copy.45), channel_id=1, replica_groups=mesh['band'=16,'ga'=2] {'band'}, dimensions={1}, use_global_device_ids=true | all-gather | bytes 696320 | tf_op jit(solution)/shard_map/all_gather | solution.py:128
  40.8 0.2 convolution_bitcast_fusion.5
  41.1 0.2 fusion.22
  41.3 0.0 all-to-all-done
  41.3 0.8 copy.50
  42.1 0.1 fusion.193
  42.3 1.9 %fusion.40 = f32[240,480]{1,0:T(8,128)S(1)} fusion(f32[160,240]{1,0:T(8,128)S(1)} %bitcast.152, f32[160]{0:T(256)S(1)} %compare_convert_fusion, s32[160]{0:T(256)S(1)} %broadcast_add_fusion), kind=kOutput, calls=%fused_computation.65 | convolution fusion | flops 221952000 | bytes 615680 | tf_op jit(solution)/shard_map/bsz,sx->bzx/dot_general | solution.py:51
  44.2 0.0 copy-start
  44.2 1.9 %fusion.41 = f32[240,480]{1,0:T(8,128)S(1)} fusion(f32[160,240]{1,0:T(8,128)S(1)} %bitcast.153, f32[160]{0:T(256)S(1)} %compare_convert_fusion, s32[160]{0:T(256)S(1)} %broadcast_add_fusion), kind=kOutput, calls=%fused_computation.66 | convolution fusion | flops 221952000 | bytes 615680 | tf_op jit(solution)/shard_map/bsz,sx->bzx/dot_general | solution.py:54
  46.1 0.0 copy-done
  46.1 1.9 %fusion.5 = f32[240,480]{1,0:T(8,128)S(1)} fusion(f32[240,480]{1,0:T(8,128)S(1)} %copy-done, f32[240,480]{1,0:T(8,128)S(1)} %fusion.40, f32[160,240]{1,0:T(8,128)S(1)} %bitcast.139, f32[160]{0:T(256)S(1)} %compare_convert_fusion, s32[160]{0:T(256)S(1)} %broadcast_add_fusion), kind=kOutput, calls=%fused_computation.8 | convolution fusion | flops 222182400 | bytes 1537280 | tf_op jit(solution)/shard_map/bsz,sx->bzx/dot_general | solution.py:53
  48.0 1.9 %fusion.39 = f32[160,240]{1,0:T(8,128)S(1)} fusion(f32[240,480]{1,0:T(8,128)S(1)} %fusion.5, f32[160]{0:T(256)S(1)} %compare_convert_fusion, s32[160]{0:T(256)S(1)} %broadcast_add_fusion), kind=kOutput, calls=%fused_computation.64 | convolution fusion | flops 221952000 | bytes 615680 | tf_op jit(solution)/shard_map/bzx,sx->bsz/dot_general | solution.py:59
  49.9 1.9 %fusion.4 = f32[240,480]{1,0:T(8,128)S(1)} fusion(f32[240,480]{1,0:T(8,128)S(1)} %copy-done, f32[240,480]{1,0:T(8,128)S(1)} %fusion.41, f32[160,240]{1,0:T(8,128)S(1)} %bitcast.140, f32[160]{0:T(256)S(1)} %compare_convert_fusion, s32[160]{0:T(256)S(1)} %broadcast_add_fusion), kind=kOutput, calls=%fused_computation.6 | convolution fusion | flops 222182400 | bytes 1537280 | tf_op jit(solution)/shard_map/bsz,sx->bzx/dot_general | solution.py:56
  51.8 1.9 %fusion.38 = f32[160,240]{1,0:T(8,128)S(1)} fusion(f32[240,480]{1,0:T(8,128)S(1)} %fusion.4, f32[160]{0:T(256)S(1)} %compare_convert_fusion, s32[160]{0:T(256)S(1)} %broadcast_add_fusion), kind=kOutput, calls=%fused_computation.63 | convolution fusion | flops 221952000 | bytes 615680 | tf_op jit(solution)/shard_map/bzx,sx->bsz/dot_general | solution.py:62
  53.7 2.1 %fusion.7 = f32[1,1,160,240]{3,2,1,0:T(8,128)S(1)} fusion(f32[160,240]{1,0:T(8,128)S(1)} %fusion.39, f32[240,480]{1,0:T(8,128)S(1)} %fusion.4, f32[160]{0:T(256)S(1)} %compare_convert_fusion, s32[160]{0:T(256)S(1)} %broadcast_add_fusion), kind=kOutput, calls=%fused_computation.12 | convolution fusion | flops 221990400 | bytes 769280 | tf_op jit(solution)/shard_map/bzx,sx->bsz/dot_general | solution.py:61
  55.9 1.9 %fusion.6 = f32[1,1,160,240]{3,2,1,0:T(8,128)S(1)} fusion(f32[160,240]{1,0:T(8,128)S(1)} %fusion.38, f32[240,480]{1,0:T(8,128)S(1)} %fusion.5, f32[160]{0:T(256)S(1)} %compare_convert_fusion, s32[160]{0:T(256)S(1)} %broadcast_add_fusion), kind=kOutput, calls=%fused_computation.10 | convolution fusion | flops 221990400 | bytes 769280 | tf_op jit(solution)/shard_map/bzx,sx->bsz/dot_general | solution.py:64
  57.8 1.1 copy.41
  58.9 3.5 %all-to-all-start.1 = ((f32[2,1,160,240]{3,1,0,2:T(1,128)}), f32[2,1,160,240]{3,1,0,2:T(1,128)S(1)}, u32[]{:S(2)}, u32[]{:S(2)}) async-start(f32[2,1,160,240]{3,1,0,2:T(1,128)} %copy.41), calls=%async_computation.1 | async-start | bytes 655360 | tf_op jit(solution)/shard_map/all_to_all | solution.py:116
  62.4 0.2 convolution_bitcast_fusion.7
  62.6 0.2 fusion.24
  62.8 6.5 %all-to-all-done.1 = f32[2,1,160,240]{3,1,0,2:T(1,128)S(1)} async-done(((f32[2,1,160,240]{3,1,0,2:T(1,128)}), f32[2,1,160,240]{3,1,0,2:T(1,128)S(1)}, u32[]{:S(2)}, u32[]{:S(2)}) %all-to-all-start.1) | async-done | bytes 307232 | tf_op jit(solution)/shard_map/all_to_all | solution.py:116
  69.3 0.2 copy.51
  69.4 0.3 copy.93
  69.7 0.1 fusion.192
  69.8 0.2 reshape.267
  70.0 1.4 %fusion.50 = f32[80,128]{1,0:T(8,128)S(1)} fusion(f32[80,480]{1,0:T(8,128)S(1)} %reshape.267, s32[128]{0:T(128)S(1)} %iota_add_fusion), kind=kOutput, calls=%fused_computation.75 | convolution fusion | flops 59535360 | bytes 195072 | tf_op jit(solution)/shard_map/bsz,pz->bsp/dot_general | solution.py:69
  71.4 0.2 reshape.268
  71.6 1.4 %fusion.48 = f32[80,128]{1,0:T(8,128)S(1)} fusion(f32[80,480]{1,0:T(8,128)S(1)} %reshape.268, s32[128]{0:T(128)S(1)} %iota_add_fusion), kind=kOutput, calls=%fused_computation.74 | convolution fusion | flops 59535360 | bytes 195072 | tf_op jit(solution)/shard_map/bsz,pz->bsp/dot_general | solution.py:72
  73.0 1.4 %fusion.16 = f32[1,80,128]{2,1,0:T(8,128)S(1)} fusion(f32[80,128]{1,0:T(8,128)S(1)} %fusion.50, f32[80,480]{1,0:T(8,128)S(1)} %reshape.268, s32[128]{0:T(128)S(1)} %iota_add_fusion), kind=kOutput, calls=%fused_computation.25 | convolution fusion | flops 59545600 | bytes 236032 | tf_op jit(solution)/shard_map/bsz,pz->bsp/dot_general | solution.py:71
  74.5 1.5 %fusion.15 = f32[1,80,128]{2,1,0:T(8,128)S(1)} fusion(f32[80,128]{1,0:T(8,128)S(1)} %fusion.48, f32[80,480]{1,0:T(8,128)S(1)} %reshape.267, s32[128]{0:T(128)S(1)} %iota_add_fusion), kind=kOutput, calls=%fused_computation.23 | convolution fusion | flops 59545600 | bytes 236032 | tf_op jit(solution)/shard_map/bsz,pz->bsp/dot_general | solution.py:74
  76.0 5.6 %fusion.14 = bf16[2,1,80,128]{3,0,2,1:T(2,128)(2,1)S(1)} fusion(s32[80,128]{1,0:T(8,128)S(1)} %get-tuple-element.16, f32[2,80,128]{2,1,0:T(8,128)S(1)} %maximum_multiply_fusion, pred[80,128]{1,0:T(8,128)(4,1)S(1)} %broadcast_compare_fusion, f32[80,128]{1,0:T(8,128)S(1)} %get-tuple-element.15, bf16[2,1,80,128]{3,2,1,0:T(8,128)(2,1)S(1)} %copy-done.1), kind=kOutput, calls=%fused_computation.21 | convolution fusion | flops 32870400 | bytes 256000 | tf_op jit(solution)/shard_map/cbsp,skp->cbsk/dot_general | solution.py:35
  81.6 0.2 convolution_bitcast_fusion.3
  81.8 0.2 convolution_bitcast_fusion.1
  82.0 0.6 copy.47
  82.7 0.2 fusion.20
  82.9 0.2 fusion.18
  83.1 4.9 %psum.7 = f32[2,2,16,1]{2,3,1,0:T(1,128)S(1)} all-reduce(f32[2,2,16,1]{2,3,1,0:T(1,128)S(1)} %pad_maximum_fusion.2), channel_id=1, replica_groups=mesh['band'=16,'ga'=2] {'ga'}, use_global_device_ids=true, to_apply=%region_0.1 | all-reduce | flops 64 | bytes 512 | tf_op jit(solution)/shard_map/psum | solution.py:133
  88.1 17.2 %all_gather.7 = f32[2,2,16,16]{2,1,0,3:T(2,128)S(1)} all-gather(f32[2,2,16,1]{2,1,0,3:T(2,128)S(1)} %bitcast.159), channel_id=1, replica_groups=mesh['band'=16,'ga'=2] {'band'}, dimensions={3}, use_global_device_ids=true | all-gather | bytes 4352 | tf_op jit(solution)/shard_map/all_gather | solution.py:134
  105.3 0.7 copy.48
  106.0 0.7 copy.49
  (14 shorter events, 0.2 us)
Async XLA Ops:
  11.9 4.4 %copy-start.2 = (s32[160]{0:T(256)S(1)}, s32[160]{0:T(256)}, u32[]{:S(2)}) copy-start(s32[160]{0:T(256)} %param.6) | copy-start | bytes 1924
  11.9 4.4 %copy-start.1 = (bf16[2,1,80,128]{3,2,1,0:T(8,128)(2,1)S(1)}, bf16[2,1,80,128]{3,2,1,0:T(8,128)(2,1)}, u32[]{:S(2)}) copy-start(bf16[2,1,80,128]{3,2,1,0:T(8,128)(2,1)} %param.4) | copy-start | bytes 122884
  11.9 29.4 %all-to-all-start = ((f32[2,1,80,480]{2,1,0,3:T(1,128)}), f32[2,1,80,480]{2,1,0,3:T(1,128)S(1)}, u32[]{:S(2)}, u32[]{:S(2)}) async-start(f32[2,1,80,480]{2,1,0,3:T(1,128)} %copy.37), calls=%async_computation | async-start | bytes 983040 | tf_op jit(solution)/shard_map/all_to_all | solution.py:114
  44.2 1.9 %copy-start = (f32[240,480]{1,0:T(8,128)S(1)}, f32[240,480]{1,0:T(8,128)}, u32[]{:S(2)}) copy-start(f32[240,480]{1,0:T(8,128)} %param.5) | copy-start | bytes 1382404
  58.9 10.4 %all-to-all-start.1 = ((f32[2,1,160,240]{3,1,0,2:T(1,128)}), f32[2,1,160,240]{3,1,0,2:T(1,128)S(1)}, u32[]{:S(2)}, u32[]{:S(2)}) async-start(f32[2,1,160,240]{3,1,0,2:T(1,128)} %copy.41), calls=%async_computation.1 | async-start | bytes 655360 | tf_op jit(solution)/shard_map/all_to_all | solution.py:116
where the time goes:
time: 107 us
  blocking collectives  46.5 us (43%)
  matrix products  37 us (35%)
  starting transfers between devices  7.82 us (7%)
  waiting for transfers between devices  6.46 us (6%)
  local copies, waits for them, and re-layouts  6.1 us (6%)
  other arithmetic  1.8 us (2%)
    all_gather x1, blocking collectives, body(): portion = lax.all_gather(masked, 'band', axis=1, tiled=True)  24.4 us
    all_gather x1, blocking collectives, body(): matrices = lax.all_gather(summed, 'band', axis=3, tiled=True)  17.2 us
    all_to_all x1, waiting for transfers between devices, body(): lax.all_to_all(gathered, 'ga', split_axis=2, concat_axis=3, tiled=True)  6.46 us
    dot_general x1, matrix products, pick_entries(): jnp.einsum('cbsp,skp->cbsk', spectra, selector.astype(jnp.float32), preci...  5.62 us
    psum x1, blocking collectives, body(): summed = lax.psum(block, 'ga')  4.93 us
    all_to_all x1, starting transfers between devices, body(): lax.all_to_all(columns, 'ga', split_axis=3, concat_axis=2, tiled=True)  4.36 us
    all_to_all x1, starting transfers between devices, body(): lax.all_to_all(gathered, 'ga', split_axis=2, concat_axis=3, tiled=True)  3.45 us
    dot_general x1, matrix products, spread_entries(): jnp.einsum('cbsk,skp->cbsp', coeffs, selector, preferred_element_type=jnp...  3.01 us
  transfers between devices with their start and end apart: 2, of which 1 were waited for; matrix products, arithmetic and copies ran while one was open for 1% of the time, Pallas kernels for 0%

commit v1 on v0

--- a/solution.py
+++ b/solution.py
@@ -113,7 +113,10 @@
     columns = z_forward(spread_entries(orbitals, own_selector), whole_cos, whole_sin)
     planes_columns = lax.all_to_all(columns, "ga", split_axis=3, concat_axis=2, tiled=True)
     gathered = plane_work(planes_columns, x_cos, x_sin, potential)
-    returned = lax.all_to_all(gathered, "ga", split_axis=2, concat_axis=3, tiled=True)
+    returned = jnp.concatenate(
+        lax.all_to_all(jnp.stack(jnp.split(gathered, lax.axis_size("ga"), axis=2)), "ga", 0, 0),
+        axis=3,
+    )
     spectra = z_backward(returned, whole_cos, whole_sin, points)
     applied = pick_entries(spectra, own_selector)
     kinetic = kinetic_factor(own_sticks, own_lists, radius)

time: 107 us -> 107 us (level)
  local copies, waits for them, and re-layouts: 6.1 us -> 4.79 us
    unnamed x10 -> x9, local copies, waits for them, and re-layouts: 2.18 us -> 2.01 us
where the time goes in v1:
time: 107 us; the launch traced here: 106 us
  blocking collectives  46.5 us (43%)
  matrix products  37 us (35%)
  starting transfers between devices  7.82 us (7%)
  waiting for transfers between devices  6.46 us (6%)
  local copies, waits for them, and re-layouts  4.79 us (4%)
  other arithmetic  2.56 us (2%)
    all_gather x1, blocking collectives, body(): portion = lax.all_gather(masked, 'band', axis=1, tiled=True)  24.4 us
    all_gather x1, blocking collectives, body(): matrices = lax.all_gather(summed, 'band', axis=3, tiled=True)  17.2 us
    all_to_all x1, waiting for transfers between devices, body(): lax.all_to_all(jnp.stack(jnp.split(gathered, lax.axis_size('ga'), axis=2)...  6.46 us
    dot_general x1, matrix products, pick_entries(): jnp.einsum('cbsp,skp->cbsk', spectra, selector.astype(jnp.float32), preci...  5.62 us
    psum x1, blocking collectives, body(): summed = lax.psum(block, 'ga')  4.93 us
    all_to_all x1, starting transfers between devices, body(): lax.all_to_all(columns, 'ga', split_axis=3, concat_axis=2, tiled=True)  4.36 us
    all_to_all x1, starting transfers between devices, body(): lax.all_to_all(jnp.stack(jnp.split(gathered, lax.axis_size('ga'), axis=2)...  3.45 us
    dot_general x1, matrix products, spread_entries(): jnp.einsum('cbsk,skp->cbsp', coeffs, selector, preferred_element_type=jnp...  3.01 us
  transfers between devices with their start and end apart: 2, of which 1 were waited for; matrix products, arithmetic and copies ran while one was open for 1% of the time, Pallas kernels for 0%

profile of v1, /device:TPU:0, one launch (start us, length us, event | category | flops | bytes accessed | tf_op | source)
XLA Modules:
  0.0 106.1 jit_solution(2580247552078738242)
XLA Ops:
  0.6 0.8 add_multiply_fusion
  1.4 0.9 convert_multiply_fusion
  2.3 3.0 %fusion.10 = f32[2,1,80,128]{3,0,2,1:T(2,128)S(1)} fusion(s32[80,128]{1,0:T(8,128)S(1)} %get-tuple-element.16, bf16[2,80,128]{2,1,0:T(8,128)(2,1)} %bitcast.160), kind=kOutput, calls=%fused_computation.17 | convolution fusion | flops 6553600 | bytes 163840 | tf_op jit(solution)/shard_map/cbsk,skp->cbsp/dot_general | solution.py:31
  5.3 0.1 fusion.197
  5.3 1.3 %fusion.54 = f32[80,480]{1,0:T(8,128)S(1)} fusion(f32[80,128]{1,0:T(8,128)S(1)} %bitcast.158, s32[128]{0:T(128)S(1)} %iota_add_fusion), kind=kOutput, calls=%fused_computation.79 | convolution fusion | flops 59535360 | bytes 195072 | tf_op jit(solution)/shard_map/bsp,pz->bsz/dot_general | solution.py:41
  6.7 1.4 %fusion.58 = f32[80,480]{1,0:T(8,128)S(1)} fusion(f32[80,128]{1,0:T(8,128)S(1)} %bitcast.159, s32[128]{0:T(128)S(1)} %iota_add_fusion), kind=kOutput, calls=%fused_computation.80 | convolution fusion | flops 59535360 | bytes 195072 | tf_op jit(solution)/shard_map/bsp,pz->bsz/dot_general | solution.py:44
  8.1 1.4 %fusion.9 = f32[1,1,80,480]{3,2,1,0:T(8,128)S(1)} fusion(f32[80,480]{1,0:T(8,128)S(1)} %fusion.54, f32[80,128]{1,0:T(8,128)S(1)} %bitcast.156, s32[128]{0:T(128)S(1)} %iota_add_fusion), kind=kOutput, calls=%fused_computation.16 | convolution fusion | flops 59573760 | bytes 348672 | tf_op jit(solution)/shard_map/bsp,pz->bsz/dot_general | solution.py:43
  9.5 1.4 %fusion.8 = f32[1,1,80,480]{3,2,1,0:T(8,128)S(1)} fusion(f32[80,480]{1,0:T(8,128)S(1)} %fusion.58, f32[80,128]{1,0:T(8,128)S(1)} %bitcast.157, s32[128]{0:T(128)S(1)} %iota_add_fusion), kind=kOutput, calls=%fused_computation.14 | convolution fusion | flops 59573760 | bytes 348672 | tf_op jit(solution)/shard_map/bsp,pz->bsz/dot_general | solution.py:46
  10.8 1.0 copy.41
  11.9 0.0 copy-start.2
  11.9 0.0 copy-start.1
  11.9 4.4 %all-to-all-start = ((f32[2,1,80,480]{2,1,0,3:T(1,128)}), f32[2,1,80,480]{2,1,0,3:T(1,128)S(1)}, u32[]{:S(2)}, u32[]{:S(2)}) async-start(f32[2,1,80,480]{2,1,0,3:T(1,128)} %copy.41), calls=%async_computation | async-start | bytes 983040 | tf_op jit(solution)/shard_map/all_to_all | solution.py:114
  16.3 0.0 copy-done.2
  16.3 0.0 copy-done.1
  16.3 0.1 broadcast_select_fusion
  16.4 24.4 %all_gather.6 = bf16[2,16,80,128]{3,2,0,1:T(8,128)(2,1)S(1)} all-gather(bf16[2,1,80,128]{3,2,0,1:T(8,128)(2,1)S(1)} %copy.50), channel_id=1, replica_groups=mesh['band'=16,'ga'=2] {'band'}, dimensions={1}, use_global_device_ids=true | all-gather | bytes 696320 | tf_op jit(solution)/shard_map/all_gather | solution.py:131
  40.8 0.2 convolution_bitcast_fusion.5
  41.1 0.2 fusion.22
  41.3 0.0 all-to-all-done
  41.3 0.8 copy.55
  42.1 0.1 fusion.196
  42.3 1.9 %fusion.42 = f32[240,480]{1,0:T(8,128)S(1)} fusion(f32[160,240]{1,0:T(8,128)S(1)} %bitcast.154, f32[160]{0:T(256)S(1)} %compare_convert_fusion, s32[160]{0:T(256)S(1)} %broadcast_add_fusion), kind=kOutput, calls=%fused_computation.69 | convolution fusion | flops 221952000 | bytes 615680 | tf_op jit(solution)/shard_map/bsz,sx->bzx/dot_general | solution.py:54
  44.2 0.0 copy-start
  44.2 1.9 %fusion.41 = f32[240,480]{1,0:T(8,128)S(1)} fusion(f32[160,240]{1,0:T(8,128)S(1)} %bitcast.155, f32[160]{0:T(256)S(1)} %compare_convert_fusion, s32[160]{0:T(256)S(1)} %broadcast_add_fusion), kind=kOutput, calls=%fused_computation.68 | convolution fusion | flops 221952000 | bytes 615680 | tf_op jit(solution)/shard_map/bsz,sx->bzx/dot_general | solution.py:51
  46.1 0.0 copy-done
  46.1 1.9 %fusion.4 = f32[240,480]{1,0:T(8,128)S(1)} fusion(f32[240,480]{1,0:T(8,128)S(1)} %copy-done, f32[240,480]{1,0:T(8,128)S(1)} %fusion.42, f32[160,240]{1,0:T(8,128)S(1)} %bitcast.142, f32[160]{0:T(256)S(1)} %compare_convert_fusion, s32[160]{0:T(256)S(1)} %broadcast_add_fusion), kind=kOutput, calls=%fused_computation.6 | convolution fusion | flops 222182400 | bytes 1537280 | tf_op jit(solution)/shard_map/bsz,sx->bzx/dot_general | solution.py:56
  48.0 1.9 %fusion.39 = f32[160,240]{1,0:T(8,128)S(1)} fusion(f32[240,480]{1,0:T(8,128)S(1)} %fusion.4, f32[160]{0:T(256)S(1)} %compare_convert_fusion, s32[160]{0:T(256)S(1)} %broadcast_add_fusion), kind=kOutput, calls=%fused_computation.66 | convolution fusion | flops 221952000 | bytes 615680 | tf_op jit(solution)/shard_map/bzx,sx->bsz/dot_general | solution.py:62
  49.9 1.9 %fusion.5 = f32[240,480]{1,0:T(8,128)S(1)} fusion(f32[240,480]{1,0:T(8,128)S(1)} %copy-done, f32[240,480]{1,0:T(8,128)S(1)} %fusion.41, f32[160,240]{1,0:T(8,128)S(1)} %bitcast.143, f32[160]{0:T(256)S(1)} %compare_convert_fusion, s32[160]{0:T(256)S(1)} %broadcast_add_fusion), kind=kOutput, calls=%fused_computation.8 | convolution fusion | flops 222182400 | bytes 1537280 | tf_op jit(solution)/shard_map/bsz,sx->bzx/dot_general | solution.py:53
  51.8 1.9 %fusion.40 = f32[160,240]{1,0:T(8,128)S(1)} fusion(f32[240,480]{1,0:T(8,128)S(1)} %fusion.5, f32[160]{0:T(256)S(1)} %compare_convert_fusion, s32[160]{0:T(256)S(1)} %broadcast_add_fusion), kind=kOutput, calls=%fused_computation.67 | convolution fusion | flops 221952000 | bytes 615680 | tf_op jit(solution)/shard_map/bzx,sx->bsz/dot_general | solution.py:59
  53.7 2.1 %fusion.6 = f32[1,1,160,240]{3,2,1,0:T(8,128)S(1)} fusion(f32[160,240]{1,0:T(8,128)S(1)} %fusion.39, f32[240,480]{1,0:T(8,128)S(1)} %fusion.5, f32[160]{0:T(256)S(1)} %compare_convert_fusion, s32[160]{0:T(256)S(1)} %broadcast_add_fusion), kind=kOutput, calls=%fused_computation.10 | convolution fusion | flops 221990400 | bytes 769280 | tf_op jit(solution)/shard_map/bzx,sx->bsz/dot_general | solution.py:64
  55.9 1.9 %fusion.7 = f32[1,1,160,240]{3,2,1,0:T(8,128)S(1)} fusion(f32[160,240]{1,0:T(8,128)S(1)} %fusion.40, f32[240,480]{1,0:T(8,128)S(1)} %fusion.4, f32[160]{0:T(256)S(1)} %compare_convert_fusion, s32[160]{0:T(256)S(1)} %broadcast_add_fusion), kind=kOutput, calls=%fused_computation.12 | convolution fusion | flops 221990400 | bytes 769280 | tf_op jit(solution)/shard_map/bzx,sx->bsz/dot_general | solution.py:61
  57.9 0.7 pad_maximum_fusion.2
  58.6 3.5 %all-to-all-start.1 = ((f32[2,2,1,80,240]{4,3,1,2,0:T(8,128)}), f32[2,2,1,80,240]{4,3,1,2,0:T(8,128)S(1)}, u32[]{:S(2)}, u32[]{:S(2)}) async-start(f32[2,2,1,80,240]{4,3,1,2,0:T(8,128)} %pad_maximum_fusion.2), calls=%async_computation.1 | async-start | bytes 655360 | tf_op jit(solution)/shard_map/all_to_all | solution.py:117
  62.1 0.2 convolution_bitcast_fusion.7
  62.3 0.2 fusion.24
  62.5 6.5 %all-to-all-done.1 = f32[2,2,1,80,240]{4,3,1,2,0:T(8,128)S(1)} async-done(((f32[2,2,1,80,240]{4,3,1,2,0:T(8,128)}), f32[2,2,1,80,240]{4,3,1,2,0:T(8,128)S(1)}, u32[]{:S(2)}, u32[]{:S(2)}) %all-to-all-start.1) | async-done | bytes 307232 | tf_op jit(solution)/shard_map/all_to_all | solution.py:117
  69.0 0.1 copy.46
  69.1 0.2 reshape.272
  69.3 1.4 %fusion.51 = f32[80,128]{1,0:T(8,128)S(1)} fusion(f32[80,480]{1,0:T(8,128)S(1)} %reshape.272, s32[128]{0:T(128)S(1)} %iota_add_fusion), kind=kOutput, calls=%fused_computation.78 | convolution fusion | flops 59535360 | bytes 195072 | tf_op jit(solution)/shard_map/bsz,pz->bsp/dot_general | solution.py:69
  70.8 0.1 copy.47
  70.9 0.2 reshape.273
  71.1 1.4 %fusion.49 = f32[80,128]{1,0:T(8,128)S(1)} fusion(f32[80,480]{1,0:T(8,128)S(1)} %reshape.273, s32[128]{0:T(128)S(1)} %iota_add_fusion), kind=kOutput, calls=%fused_computation.77 | convolution fusion | flops 59535360 | bytes 195072 | tf_op jit(solution)/shard_map/bsz,pz->bsp/dot_general | solution.py:72
  72.5 1.4 %fusion.16 = f32[1,80,128]{2,1,0:T(8,128)S(1)} fusion(f32[80,128]{1,0:T(8,128)S(1)} %fusion.51, f32[80,480]{1,0:T(8,128)S(1)} %reshape.273, s32[128]{0:T(128)S(1)} %iota_add_fusion), kind=kOutput, calls=%fused_computation.25 | convolution fusion | flops 59545600 | bytes 236032 | tf_op jit(solution)/shard_map/bsz,pz->bsp/dot_general | solution.py:71
  73.9 1.5 %fusion.15 = f32[1,80,128]{2,1,0:T(8,128)S(1)} fusion(f32[80,128]{1,0:T(8,128)S(1)} %fusion.49, f32[80,480]{1,0:T(8,128)S(1)} %reshape.272, s32[128]{0:T(128)S(1)} %iota_add_fusion), kind=kOutput, calls=%fused_computation.23 | convolution fusion | flops 59545600 | bytes 236032 | tf_op jit(solution)/shard_map/bsz,pz->bsp/dot_general | solution.py:74
  75.4 5.6 %fusion.14 = bf16[2,1,80,128]{3,0,2,1:T(2,128)(2,1)S(1)} fusion(s32[80,128]{1,0:T(8,128)S(1)} %get-tuple-element.16, f32[2,80,128]{2,1,0:T(8,128)S(1)} %maximum_multiply_fusion, pred[80,128]{1,0:T(8,128)(4,1)S(1)} %broadcast_compare_fusion, f32[80,128]{1,0:T(8,128)S(1)} %get-tuple-element.15, bf16[2,1,80,128]{3,2,1,0:T(8,128)(2,1)S(1)} %copy-done.1), kind=kOutput, calls=%fused_computation.21 | convolution fusion | flops 32870400 | bytes 256000 | tf_op jit(solution)/shard_map/cbsp,skp->cbsk/dot_general | solution.py:35
  81.0 0.2 convolution_bitcast_fusion.3
  81.3 0.2 convolution_bitcast_fusion.1
  81.5 0.6 copy.52
  82.1 0.2 fusion.20
  82.3 0.2 fusion.18
  82.6 4.9 %psum.7 = f32[2,2,16,1]{2,3,1,0:T(1,128)S(1)} all-reduce(f32[2,2,16,1]{2,3,1,0:T(1,128)S(1)} %pad_maximum_fusion.3), channel_id=1, replica_groups=mesh['band'=16,'ga'=2] {'ga'}, use_global_device_ids=true, to_apply=%region_0.1 | all-reduce | flops 64 | bytes 512 | tf_op jit(solution)/shard_map/psum | solution.py:136
  87.5 17.2 %all_gather.7 = f32[2,2,16,16]{2,1,0,3:T(2,128)S(1)} all-gather(f32[2,2,16,1]{2,1,0,3:T(2,128)S(1)} %bitcast.161), channel_id=1, replica_groups=mesh['band'=16,'ga'=2] {'band'}, dimensions={3}, use_global_device_ids=true | all-gather | bytes 4352 | tf_op jit(solution)/shard_map/all_gather | solution.py:137
  104.7 0.7 copy.53
  105.4 0.7 copy.54
  (17 shorter events, 0.2 us)
Async XLA Ops:
  11.9 4.4 %copy-start.2 = (s32[160]{0:T(256)S(1)}, s32[160]{0:T(256)}, u32[]{:S(2)}) copy-start(s32[160]{0:T(256)} %param.6) | copy-start | bytes 1924
  11.9 4.4 %copy-start.1 = (bf16[2,1,80,128]{3,2,1,0:T(8,128)(2,1)S(1)}, bf16[2,1,80,128]{3,2,1,0:T(8,128)(2,1)}, u32[]{:S(2)}) copy-start(bf16[2,1,80,128]{3,2,1,0:T(8,128)(2,1)} %param.4) | copy-start | bytes 122884
  11.9 29.4 %all-to-all-start = ((f32[2,1,80,480]{2,1,0,3:T(1,128)}), f32[2,1,80,480]{2,1,0,3:T(1,128)S(1)}, u32[]{:S(2)}, u32[]{:S(2)}) async-start(f32[2,1,80,480]{2,1,0,3:T(1,128)} %copy.41), calls=%async_computation | async-start | bytes 983040 | tf_op jit(solution)/shard_map/all_to_all | solution.py:114
  44.2 1.9 %copy-start = (f32[240,480]{1,0:T(8,128)S(1)}, f32[240,480]{1,0:T(8,128)}, u32[]{:S(2)}) copy-start(f32[240,480]{1,0:T(8,128)} %param.5) | copy-start | bytes 1382404
  58.6 10.4 %all-to-all-start.1 = ((f32[2,2,1,80,240]{4,3,1,2,0:T(8,128)}), f32[2,2,1,80,240]{4,3,1,2,0:T(8,128)S(1)}, u32[]{:S(2)}, u32[]{:S(2)}) async-start(f32[2,2,1,80,240]{4,3,1,2,0:T(8,128)} %pad_maximum_fusion.2), calls=%async_computation.1 | async-start | bytes 655360 | tf_op jit(solution)/shard_map/all_to_all | solution.py:117
